TPU v7x, 32 devices: a whole 2x2x4 slice. The times are simulated.
32 devices in a mesh: groups: 2 (over y), seq: 8 (over z, core), side: 1, req: 2 (over x).
Axes of the slice: x: 2, y: 2, z: 4, core: 2. Of those that a mesh axis runs over, the one named last changes fastest.
Arguments:
- queries: bfloat16 [4, 128, 4, 2048], P(('groups', 'req'), 'seq', 'side'), parts along dimension 0, may hold values from -8 to 8
- cache_keys: bfloat16 [4, 1024, 512], P(('groups', 'req'), 'seq', 'side'), parts along dimension 0, may hold values from -8 to 8
- cache_values: bfloat16 [4, 1024, 512], P(('groups', 'req'), 'seq', 'side'), parts along dimension 0, may hold values from -6 to 6
- tree_keys: bfloat16 [4, 128, 512], P(('groups', 'req'), 'seq', 'side'), parts along dimension 0, may hold values from -8 to 8
- tree_values: bfloat16 [4, 128, 512], P(('groups', 'req'), 'seq', 'side'), parts along dimension 0, may hold values from -6 to 6
- parents: int32 [4, 128], P(('groups', 'req')), parts along dimension 0, may hold values from 0 to 126, as said below
- lengths: int32 [4], P(('groups', 'req')), parts along dimension 0, may hold values from 128 to 1024
- out_weight: bfloat16 [4, 2048, 4096], P('side', 'seq', 'req'), may hold values from -0.0625 to 0.0625
- in_experts: bfloat16 [64, 4096, 1024], P(('seq', 'side'), 'req'), may hold values from -0.09375 to 0.09375
- out_experts: bfloat16 [64, 1024, 4096], P(('seq', 'side'), None, 'req'), may hold values from -0.1875 to 0.1875
- gate_experts: int32 [512, 8], P(('groups', 'seq', 'side')), parts along dimension 0, may hold values from 0 to 63, all different within a row; in each aligned block of 32 rows (0 to 31, 32 to 63, ...) at most 6 rows name the same one
- gate_weights: float32 [512, 8], P(('groups', 'seq', 'side')), parts along dimension 0, may hold values from 0.1 to 1
Outputs:
- attended: bfloat16 [512, 4096], P(('groups', 'seq', 'side'), 'req'), parts along dimension 0
- expert_out: bfloat16 [512, 4096], P(('groups', 'seq', 'side'), 'req'), parts along dimension 0
There are 2 independent parts, one for each index of `groups`. A program takes and returns all parts, laid end to end along the dimension named above; an argument that names none is the same for every part. Nothing has to cross between parts.
Inputs may be any that keep to these rules, and one draw needn't show every extreme that they name: parents[r, 0] is 0; every node i >= 1 has its parent among nodes i - 4 to i - 1. `gate_experts`: within the 32 rows that one device holds along seq+side, no expert is named by more than 6 rows, and in some such block one expert is named exactly 6 times.
All inputs are finite; a program needn't handle non-finite values.
Results may differ from a plain program's by a relative error of at most 0.018.
Values may be sent and summed in bfloat16 or wider, within the bound.
No kernel may reach another device: no remote copies, remote signals or barrier semaphores. Data moves between devices by JAX's collectives and lax.ppermute only.
A program may use at most 128 MiB of HBM per device.

v0:
```python
import math
import jax
import jax.numpy as jnp
from jax import lax
from jax.sharding import PartitionSpec as P

GROUP = 16
HD = 128
EXPERTS = 64
CAP = 6
NEG_FILL = -1e30


def ancestors(parent_row, node_count):
    node_ids = jnp.arange(node_count, dtype=jnp.int32)
    parent_hit = (node_ids[None, :] == parent_row[:, None]).astype(jnp.float32)
    reached = jnp.maximum(parent_hit, jnp.eye(node_count, dtype=jnp.float32))
    for turn_number in range(max(1, (node_count - 1).bit_length())):
        reached = jnp.minimum(jnp.dot(reached, reached, precision=lax.Precision.HIGHEST), 1.0)
    return reached


def per_device(
    queries,
    cache_keys,
    cache_values,
    tree_keys,
    tree_values,
    parents,
    lengths,
    out_weight,
    in_experts,
    out_experts,
    gate_experts,
    gate_weights,
):
    seq_index = lax.axis_index("seq")
    ctx_local = cache_keys.shape[1]
    nodes_local = queries.shape[1]
    kv_local = queries.shape[2]
    gathered = lax.all_gather(queries, "seq", axis=1, tiled=True)
    node_count = gathered.shape[1]
    reached = ancestors(parents[0], node_count)
    tree_seen = lax.dynamic_slice_in_dim(reached, seq_index * nodes_local, nodes_local, 1) > 0.5
    positions = seq_index * ctx_local + jnp.arange(ctx_local, dtype=jnp.int32)
    context_seen = jnp.broadcast_to((positions < lengths[0])[None, :], (node_count, ctx_local))
    visible = jnp.concatenate([context_seen, tree_seen], axis=1)[None]
    factor = 1.0 / math.sqrt(HD)
    outputs, maxima, totals = ([], [], [])
    for head_pair in range(kv_local):
        first_col = head_pair * HD
        key_rows = jnp.concatenate(
            [
                cache_keys[0, :, first_col : first_col + HD],
                tree_keys[0, :, first_col : first_col + HD],
            ],
            axis=0,
        )
        value_rows = jnp.concatenate(
            [
                cache_values[0, :, first_col : first_col + HD],
                tree_values[0, :, first_col : first_col + HD],
            ],
            axis=0,
        )
        query_block = gathered[0, :, head_pair].reshape(node_count, GROUP, HD)
        scores = (
            jnp.einsum("ngd,kd->gnk", query_block, key_rows, preferred_element_type=jnp.float32)
            * factor
        )
        masked = jnp.where(visible, scores, NEG_FILL)
        row_max = jnp.max(masked, axis=-1)
        weights = jnp.where(visible, jnp.exp(masked - row_max[..., None]), 0.0)
        weights_low = weights.astype(jnp.bfloat16)
        outputs.append(
            jnp.einsum("gnk,kd->gnd", weights_low, value_rows, preferred_element_type=jnp.float32)
        )
        maxima.append(row_max)
        totals.append(jnp.sum(weights, axis=-1))
    partial_out = jnp.stack(outputs)
    partial_max = jnp.stack(maxima)
    partial_sum = jnp.stack(totals)
    pieces = (
        lax.all_to_all(partial_out[None], "seq", split_axis=2, concat_axis=0, tiled=True),
        lax.all_to_all(partial_max[None], "seq", split_axis=2, concat_axis=0, tiled=True),
        lax.all_to_all(partial_sum[None], "seq", split_axis=2, concat_axis=0, tiled=True),
    )
    larger = jnp.max(pieces[1], axis=0)
    scales = jnp.exp(pieces[1] - larger[None])
    merged = jnp.sum(pieces[0] * scales[..., None], axis=0)
    summed = jnp.sum(pieces[2] * scales, axis=0)
    attention = merged / summed[..., None]
    attention = jnp.transpose(attention, (2, 0, 1, 3)).reshape(node_count, -1).astype(jnp.bfloat16)
    head_rows = lax.all_gather(attention, "req", axis=0, tiled=True)
    projector = out_weight.reshape(-1, out_weight.shape[2])
    attended = lax.psum_scatter(
        jnp.dot(head_rows, projector, preferred_element_type=jnp.float32),
        ("seq", "side"),
        scatter_dimension=0,
        tiled=True,
    ).astype(jnp.bfloat16)
    local_experts = in_experts.shape[0]
    flat_ids = gate_experts.reshape(-1)
    expert_hit = (flat_ids[:, None] == jnp.arange(EXPERTS, dtype=jnp.int32)[None, :]).astype(
        jnp.int32
    )
    earlier = jnp.cumsum(expert_hit, axis=0) - expert_hit
    slot_rank = jnp.sum(earlier * expert_hit, axis=1)
    slot_ids = (flat_ids * CAP + slot_rank).reshape(gate_experts.shape)
    slot_count = EXPERTS * CAP
    matches = jnp.arange(slot_count, dtype=jnp.int32)[:, None, None] == slot_ids[None]
    placing = jnp.any(matches, axis=2).astype(jnp.bfloat16)
    mixing = jnp.sum(jnp.where(matches, gate_weights[None], 0.0), axis=2)
    outgoing = jnp.dot(placing, attended, preferred_element_type=jnp.float32).astype(jnp.bfloat16)
    device_count = EXPERTS // local_experts
    outgoing = outgoing.reshape(device_count, local_experts, CAP, -1)
    before = jnp.einsum(
        "sekd,edf->sekf",
        lax.all_to_all(outgoing, ("seq", "side"), split_axis=0, concat_axis=0, tiled=True),
        in_experts,
        preferred_element_type=jnp.float32,
    )
    hidden_sum = lax.psum(before, "req")
    hidden = jax.nn.silu(hidden_sum).astype(jnp.bfloat16)
    produced = jnp.einsum(
        "sekf,efd->sekd", hidden, out_experts, preferred_element_type=jnp.float32
    ).astype(jnp.bfloat16)
    came_back = lax.all_to_all(produced, ("seq", "side"), split_axis=0, concat_axis=0, tiled=True)
    slot_rows = came_back.reshape(slot_count, -1).astype(jnp.float32)
    expert_mix = jnp.dot(mixing.T, slot_rows, precision=lax.Precision.HIGHEST)
    return (attended, expert_mix.astype(jnp.bfloat16))


def solution(mesh):
    placed = (
        P(("groups", "req"), "seq", "side", None),
        P(("groups", "req"), "seq", "side"),
        P(("groups", "req"), "seq", "side"),
        P(("groups", "req"), "seq", "side"),
        P(("groups", "req"), "seq", "side"),
        P(("groups", "req"), None),
        P(("groups", "req")),
        P("side", "seq", "req"),
        P(("seq", "side"), "req", None),
        P(("seq", "side"), None, "req"),
        P(("groups", "seq", "side"), None),
        P(("groups", "seq", "side"), None),
    )
    return jax.shard_map(
        per_device,
        mesh=mesh,
        in_specs=placed,
        out_specs=(P(("groups", "seq", "side"), "req"), P(("groups", "seq", "side"), "req")),
        check_vma=False,
    )
```

profile of v0, /device:TPU:0, one launch (start us, length us, event | category | flops | bytes accessed | tf_op | source)
XLA Modules:
  0.0 424.0 jit_solution(3540894547488860294)
XLA Ops:
  13.6 27.9 %all-gather.2.cloned.1.call-done = bf16[1,128,4,2048]{3,2,0,1:T(4,128)(2,1)} async-done(((bf16[1,16,4,2048]{3,2,0,1:T(4,128)(2,1)}), bf16[1,128,4,2048]{3,2,0,1:T(4,128)(2,1)}) %all-gather.2.cloned.1.call-update) | async-done | bytes 2097168 | tf_op jit(solution)/shard_map/all_gather | solution.py:41
  41.6 9.0 %fusion.90 = (bf16[1,128,1,2048]{3,2,0,1:T(2,128)(2,1)S(1)}, bf16[1,128,1,2048]{3,2,0,1:T(2,128)(2,1)}, bf16[1,128,1,2048]{3,2,0,1:T(2,128)(2,1)S(1)}, bf16[1,128,1,2048]{3,2,0,1:T(2,128)(2,1)S(1)}) fusion(bf16[1,128,4,2048]{3,2,0,1:T(4,128)(2,1)} %all-gather.2.cloned.1.call-done), kind=kLoop, calls=%fused_computation.143 | loop fusion | bytes 4194304 | tf_op jit(solution)/shard_map/slice | solution.py:66
  50.5 3.5 copy.144
  64.0 4.0 all-to-all-start.2
  68.0 2.8 convolution_bitcast_fusion.3
  76.0 5.0 %all-to-all-start.1 = ((f32[1,4,16,128]{3,1,0,2:T(4,128)}), f32[1,4,16,128]{3,1,0,2:T(4,128)S(1)}, u32[]{:S(2)}, u32[]{:S(2)}) async-start(f32[1,4,16,128]{3,1,0,2:T(4,128)} %maximum_bitcast_fusion.17), calls=%async_computation.1 | async-start | bytes 65536 | tf_op jit(solution)/shard_map/all_to_all | solution.py:85
  81.1 1.9 maximum_bitcast_fusion
  83.0 2.2 copy.116
  86.8 4.5 %all-to-all-start = ((f32[1,4,16,128,128]{4,3,1,0,2:T(8,128)}), f32[1,4,16,128,128]{4,3,1,0,2:T(8,128)}, u32[]{:S(2)}, u32[]{:S(2)}) async-start(f32[1,4,16,128,128]{4,3,1,0,2:T(8,128)} %copy.116), calls=%async_computation | async-start | bytes 8388608 | tf_op jit(solution)/shard_map/all_to_all | solution.py:84
  92.2 93.1 %all-to-all-done = f32[1,4,16,128,128]{4,3,1,0,2:T(8,128)} async-done(((f32[1,4,16,128,128]{4,3,1,0,2:T(8,128)}), f32[1,4,16,128,128]{4,3,1,0,2:T(8,128)}, u32[]{:S(2)}, u32[]{:S(2)}) %all-to-all-start) | async-done | bytes 4194336 | tf_op jit(solution)/shard_map/all_to_all | solution.py:84
  185.3 2.9 fusion.4
  188.6 8.5 %all_gather.7 = bf16[256,1024]{0,1:T(8,128)(2,1)S(1)} all-gather(bf16[128,1024]{0,1:T(8,128)(2,1)S(1)} %bitcast.199), channel_id=1, replica_groups=mesh['groups'=2,'seq'=8,'side'=1,'req'=2] {'req'}, dimensions={0}, use_global_device_ids=true | all-gather | bytes 786432 | tf_op jit(solution)/shard_map/all_gather | solution.py:94
  197.1 4.8 %fusion.96 = f32[256,2048]{1,0:T(8,128)} fusion(bf16[256,1024]{0,1:T(8,128)(2,1)S(1)} %all_gather.7, bf16[1024,2048]{1,0:T(8,128)(2,1)} %bitcast.212), kind=kOutput, calls=%fused_computation.149 | convolution fusion | flops 1073741824 | bytes 6815744 | tf_op jit(solution)/shard_map/dot_general | solution.py:97
  204.1 33.4 %reduce-scatter.2.cloned.1.call-done = f32[32,2048]{1,0:T(8,128)} async-done(((f32[256,2048]{1,0:T(8,128)}), f32[32,2048]{1,0:T(8,128)}) %reduce-scatter.2.cloned.1.call-update) | async-done | bytes 262160 | tf_op jit(solution)/shard_map/reduce_scatter | solution.py:96
  240.3 2.5 reshape.61
  243.7 40.2 %all_to_all.64 = bf16[8,8,6,2048]{3,1,2,0:T(8,128)(2,1)S(1)} all-to-all(bf16[8,8,6,2048]{3,1,2,0:T(8,128)(2,1)S(1)} %copy.126), channel_id=1, replica_groups=mesh['groups'=2,'seq'=8,'side'=1,'req'=2] {'seq','side'}, dimensions={0} | all-to-all | bytes 3145728 | tf_op jit(solution)/shard_map/all_to_all | solution.py:119
  283.9 14.8 %fusion.12 = f32[8,8,6,1024]{3,0,2,1:T(8,128)} fusion(bf16[8,2048,1024]{2,1,0:T(8,128)(2,1)} %param.20, bf16[8,8,6,2048]{3,1,2,0:T(8,128)(2,1)S(1)} %all_to_all.64), kind=kOutput, calls=%fused_computation.13 | convolution fusion | flops 1610612736 | bytes 36700160 | tf_op jit(solution)/shard_map/sekd,edf->sekf/dot_general | solution.py:117
  298.7 50.5 %all-reduce.2.cloned.1.call-done = f32[8,8,6,1024]{3,0,2,1:T(8,128)} async-done(((f32[8,8,6,1024]{3,0,2,1:T(8,128)}), f32[8,8,6,1024]{3,0,2,1:T(8,128)}) %all-reduce.2.cloned.1.call-update) | async-done | bytes 1572880 | tf_op jit(solution)/shard_map/psum | solution.py:123
  349.3 16.9 %fusion.8 = bf16[8,8,6,2048]{3,0,2,1:T(8,128)(2,1)S(1)} fusion(bf16[8,1024,2048]{2,1,0:T(8,128)(2,1)} %param.21, f32[8,8,6,1024]{3,0,2,1:T(8,128)} %all-reduce.2.cloned.1.call-done), kind=kOutput, calls=%fused_computation.9 | convolution fusion | flops 1613365248 | bytes 36700160 | tf_op jit(solution)/shard_map/sekf,efd->sekd/dot_general | solution.py:125
  366.2 2.0 copy.128
  368.2 4.7 %all-to-all-start.4 = ((bf16[8,8,6,2048]{3,1,2,0:T(8,128)(2,1)}), bf16[8,8,6,2048]{3,1,2,0:T(8,128)(2,1)}, u32[]{:S(2)}, u32[]{:S(2)}) async-start(bf16[8,8,6,2048]{3,1,2,0:T(8,128)(2,1)} %copy.128), calls=%async_computation.5 | async-start | bytes 3145728 | tf_op jit(solution)/shard_map/all_to_all | solution.py:128
  373.2 37.6 %all-to-all-done.4 = bf16[8,8,6,2048]{3,1,2,0:T(8,128)(2,1)} async-done(((bf16[8,8,6,2048]{3,1,2,0:T(8,128)(2,1)}), bf16[8,8,6,2048]{3,1,2,0:T(8,128)(2,1)}, u32[]{:S(2)}, u32[]{:S(2)}) %all-to-all-start.4) | async-done | bytes 1572896 | tf_op jit(solution)/shard_map/all_to_all | solution.py:128
  410.8 2.3 copy.129
  414.6 2.9 convolution_convert_fusion.1
  (116 shorter events, 31.0 us)
Async XLA Ops:
  7.2 3.9 copy-start.24
  7.2 4.5 %copy-start.25 = (bf16[1,16,512]{2,1,0:T(8,128)(2,1)S(1)}, bf16[1,16,512]{2,1,0:T(8,128)(2,1)}, u32[]{:S(2)}) copy-start(bf16[1,16,512]{2,1,0:T(8,128)(2,1)} %param.16) | copy-start | bytes 49156
  7.2 5.1 %copy-start.14 = (bf16[1,128,512]{2,1,0:T(8,128)(2,1)S(1)}, bf16[1,128,512]{2,1,0:T(8,128)(2,1)}, u32[]{:S(2)}) copy-start(bf16[1,128,512]{2,1,0:T(8,128)(2,1)} %param.13) | copy-start | bytes 393220
  7.2 5.8 %copy-start.15 = (bf16[1,128,512]{2,1,0:T(8,128)(2,1)S(1)}, bf16[1,128,512]{2,1,0:T(8,128)(2,1)}, u32[]{:S(2)}) copy-start(bf16[1,128,512]{2,1,0:T(8,128)(2,1)} %param.14) | copy-start | bytes 393220
  7.2 34.3 %all-gather.2.cloned.1.call-start = ((), (), s32[]{:S(2)}) async-start(), calls=%async_computation.6 | async-start | bytes 2359296 | tf_op jit(solution)/shard_map/all_gather | solution.py:41
  11.1 49.0 %copy-start.6 = (pred[128,144]{0,1:T(8,128)(4,1)}, pred[128,144]{0,1:T(8,128)(4,1)S(1)}, u32[]{:S(2)}) copy-start(pred[128,144]{0,1:T(8,128)(4,1)S(1)} %pad_add_fusion) | copy-start | bytes 55300
  56.8 1.9 copy-start.5
  60.4 2.9 copy-start
  60.4 2.9 copy-start.10
  60.4 1.7 copy-start.7
  64.0 12.1 %all-to-all-start.2 = ((f32[1,4,16,128]{3,1,0,2:T(4,128)}), f32[1,4,16,128]{3,1,0,2:T(4,128)}, u32[]{:S(2)}, u32[]{:S(2)}) async-start(f32[1,4,16,128]{3,1,0,2:T(4,128)} %maximum_bitcast_fusion.18), calls=%async_computation.2 | async-start | bytes 65536 | tf_op jit(solution)/shard_map/all_to_all | solution.py:86
  67.9 2.9 copy-start.8
  67.9 2.9 copy-start.19
  68.0 2.9 copy-start.22
  70.8 1.5 copy-start.21
  73.9 7.2 %copy-start.1 = (f32[1,16,128,128]{3,2,1,0:T(8,128)S(1)}, f32[1,16,128,128]{3,2,1,0:T(8,128)}, u32[]{:S(2)}) copy-start(f32[1,16,128,128]{3,2,1,0:T(8,128)} %convolution_bitcast_fusion.3) | copy-start | bytes 3145732
  73.9 7.2 %copy-start.2 = (f32[1,16,128,128]{3,2,1,0:T(8,128)S(1)}, f32[1,16,128,128]{3,2,1,0:T(8,128)}, u32[]{:S(2)}) copy-start(f32[1,16,128,128]{3,2,1,0:T(8,128)} %convolution_bitcast_fusion.2) | copy-start | bytes 3145732
  76.0 10.7 %all-to-all-start.1 = ((f32[1,4,16,128]{3,1,0,2:T(4,128)}), f32[1,4,16,128]{3,1,0,2:T(4,128)S(1)}, u32[]{:S(2)}, u32[]{:S(2)}) async-start(f32[1,4,16,128]{3,1,0,2:T(4,128)} %maximum_bitcast_fusion.17), calls=%async_computation.1 | async-start | bytes 65536 | tf_op jit(solution)/shard_map/all_to_all | solution.py:85
  86.8 98.5 %all-to-all-start = ((f32[1,4,16,128,128]{4,3,1,0,2:T(8,128)}), f32[1,4,16,128,128]{4,3,1,0,2:T(8,128)}, u32[]{:S(2)}, u32[]{:S(2)}) async-start(f32[1,4,16,128,128]{4,3,1,0,2:T(8,128)} %copy.116), calls=%async_computation | async-start | bytes 8388608 | tf_op jit(solution)/shard_map/all_to_all | solution.py:84
  91.3 146.2 %reduce-scatter.2.cloned.1.call-start = ((), (), s32[]{:S(2)}) async-start(), calls=%async_computation.7 | async-start | bytes 2359296 | tf_op jit(solution)/shard_map/reduce_scatter | solution.py:96
  201.9 147.4 %all-reduce.2.cloned.1.call-start = ((), (), s32[]{:S(2)}) async-start(), calls=%async_computation.8 | async-start | bytes 3145728 | tf_op jit(solution)/shard_map/psum | solution.py:123
  238.5 4.3 %copy-start.9 = (bf16[32,2048]{1,0:T(8,128)(2,1)}, bf16[32,2048]{1,0:T(8,128)(2,1)S(1)}, u32[]{:S(2)}) copy-start(bf16[32,2048]{1,0:T(8,128)(2,1)S(1)} %convert_element_type.59) | copy-start | bytes 393220
  368.2 4.7 %copy-start.27 = (f32[32,8]{0,1:T(8,128)S(1)}, f32[32,8]{0,1:T(8,128)}, u32[]{:S(2)}) copy-start(f32[32,8]{0,1:T(8,128)} %param.23) | copy-start | bytes 3076
  368.2 42.6 %all-to-all-start.4 = ((bf16[8,8,6,2048]{3,1,2,0:T(8,128)(2,1)}), bf16[8,8,6,2048]{3,1,2,0:T(8,128)(2,1)}, u32[]{:S(2)}, u32[]{:S(2)}) async-start(bf16[8,8,6,2048]{3,1,2,0:T(8,128)(2,1)} %copy.128), calls=%async_computation.5 | async-start | bytes 3145728 | tf_op jit(solution)/shard_map/all_to_all | solution.py:128
  (11 other events, 13.7 us)
Sparse Core Ops, SparseCore 0:
  9.6 31.8 all-gather.1
  202.0 35.4 reduce-scatter.1
  298.8 50.3 all-reduce.1
where the time goes:
time: 425 us; the launch traced here: 424 us
  waiting for transfers between devices  245 us (58%)
  matrix products  52.8 us (12%)
  blocking collectives  48.7 us (11%)
  local copies, waits for them, and re-layouts  33.7 us (8%)
  starting transfers between devices  18.5 us (4%)
  between operations  14.9 us (4%)
  other arithmetic  10.5 us (2%)
    all_to_all x1, waiting for transfers between devices, per_device(): lax.all_to_all(partial_out[None], 'seq', split_axis=2, concat_axis=0, til...  93.1 us
    psum x1, waiting for transfers between devices, per_device(): hidden_sum = lax.psum(before, 'req')  50.5 us
    all_to_all x1, blocking collectives, per_device(): lax.all_to_all(outgoing, ('seq', 'side'), split_axis=0, concat_axis=0, ti...  40.2 us
    all_to_all x1, waiting for transfers between devices, per_device(): lax.all_to_all(produced, ('seq', 'side'), split_axis=0, concat_axis=0, ti...  37.6 us
    reduce_scatter x1, waiting for transfers between devices, per_device(): lax.psum_scatter(jnp.dot(head_rows, projector, preferred_element_type=jnp...  33.4 us
    all_gather x1, waiting for transfers between devices, per_device(): gathered = lax.all_gather(queries, 'seq', axis=1, tiled=True)  27.9 us
    dot_general x1, matrix products, per_device(): jnp.einsum('sekf,efd->sekd', hidden, out_experts, preferred_element_type=...  16.9 us
    dot_general x1, matrix products, per_device(): jnp.einsum('sekd,edf->sekf', lax.all_to_all(outgoing, ('seq', 'side'), sp...  14.8 us
  transfers between devices with their start and end apart: 7, of which 6 were waited for; matrix products, arithmetic and copies ran while one was open for 5% of the time, Pallas kernels for 0%

commit v1 on v0

--- a/solution.py
+++ b/solution.py
@@ -38,7 +38,7 @@
     ctx_local = cache_keys.shape[1]
     nodes_local = queries.shape[1]
     kv_local = queries.shape[2]
-    gathered = lax.all_gather(queries, "seq", axis=1, tiled=True)
+    gathered = jnp.concatenate(lax.all_gather(queries, "seq"), axis=1)
     node_count = gathered.shape[1]
     reached = ancestors(parents[0], node_count)
     tree_seen = lax.dynamic_slice_in_dim(reached, seq_index * nodes_local, nodes_local, 1) > 0.5

time: 425 us -> 410 us (0.965)
  local copies, waits for them, and re-layouts: 33.7 us -> 21.9 us
    unnamed x62 -> x63, local copies, waits for them, and re-layouts: 10.1 us -> 3.81 us
    slice x1 -> x5, local copies, waits for them, and re-layouts: 8.99 us -> 3.5 us  [per_device(): query_block = gathered[0, :, head_pair].reshape(node_count, GROUP, HD)]
  transfers between devices with their start and end apart: 7 -> 7, of which waited for: 6 -> 6; matrix products, arithmetic and copies ran while one was open for 5% -> 4% of each run, Pallas kernels for 0% -> 0%
where the time goes in v1:
time: 410 us; the launch traced here: 409 us
  waiting for transfers between devices  243 us (59%)
  matrix products  51.4 us (13%)
  blocking collectives  48.7 us (12%)
  local copies, waits for them, and re-layouts  21.9 us (5%)
  starting transfers between devices  18.5 us (5%)
  between operations  15 us (4%)
  other arithmetic  10.5 us (3%)
    all_to_all x1, waiting for transfers between devices, per_device(): lax.all_to_all(partial_out[None], 'seq', split_axis=2, concat_axis=0, til...  93.1 us
    psum x1, waiting for transfers between devices, per_device(): hidden_sum = lax.psum(before, 'req')  50.5 us
    all_to_all x1, blocking collectives, per_device(): lax.all_to_all(outgoing, ('seq', 'side'), split_axis=0, concat_axis=0, ti...  40.2 us
    all_to_all x1, waiting for transfers between devices, per_device(): lax.all_to_all(produced, ('seq', 'side'), split_axis=0, concat_axis=0, ti...  37.6 us
    reduce_scatter x1, waiting for transfers between devices, per_device(): lax.psum_scatter(jnp.dot(head_rows, projector, preferred_element_type=jnp...  33.4 us
    all_gather x1, waiting for transfers between devices, per_device(): gathered = jnp.concatenate(lax.all_gather(queries, 'seq'), axis=1)  26.7 us
    dot_general x1, matrix products, per_device(): jnp.einsum('sekf,efd->sekd', hidden, out_experts, preferred_element_type=...  16.9 us
    dot_general x1, matrix products, per_device(): jnp.einsum('sekd,edf->sekf', lax.all_to_all(outgoing, ('seq', 'side'), sp...  14.8 us
  transfers between devices with their start and end apart: 7, of which 6 were waited for; matrix products, arithmetic and copies ran while one was open for 4% of the time, Pallas kernels for 0%

profile of v1, /device:TPU:0, one launch (start us, length us, event | category | flops | bytes accessed | tf_op | source)
XLA Modules:
  0.0 408.8 jit_solution(16134296569815156268)
XLA Ops:
  7.3 1.9 copy.125
  14.9 26.7 %all-gather.3.cloned.1.call-done = bf16[8,16,4,2048]{3,1,0,2:T(8,128)(2,1)} async-done(((bf16[1,16,4,2048]{3,1,0,2:T(8,128)(2,1)}), bf16[8,16,4,2048]{3,1,0,2:T(8,128)(2,1)}) %all-gather.3.cloned.1.call-update) | async-done | bytes 2097168 | tf_op jit(solution)/shard_map/all_gather | solution.py:41
  50.1 4.0 all-to-all-start.2
  54.1 2.4 convolution_bitcast_fusion.2
  60.9 5.0 %all-to-all-start.1 = ((f32[1,4,16,128]{3,1,0,2:T(4,128)}), f32[1,4,16,128]{3,1,0,2:T(4,128)S(1)}, u32[]{:S(2)}, u32[]{:S(2)}) async-start(f32[1,4,16,128]{3,1,0,2:T(4,128)} %maximum_bitcast_fusion.17), calls=%async_computation.1 | async-start | bytes 65536 | tf_op jit(solution)/shard_map/all_to_all | solution.py:85
  65.9 1.9 maximum_bitcast_fusion
  67.8 2.2 copy.134
  71.7 4.5 %all-to-all-start = ((f32[1,4,16,128,128]{4,3,1,0,2:T(8,128)}), f32[1,4,16,128,128]{4,3,1,0,2:T(8,128)}, u32[]{:S(2)}, u32[]{:S(2)}) async-start(f32[1,4,16,128,128]{4,3,1,0,2:T(8,128)} %copy.134), calls=%async_computation | async-start | bytes 8388608 | tf_op jit(solution)/shard_map/all_to_all | solution.py:84
  77.1 93.1 %all-to-all-done = f32[1,4,16,128,128]{4,3,1,0,2:T(8,128)} async-done(((f32[1,4,16,128,128]{4,3,1,0,2:T(8,128)}), f32[1,4,16,128,128]{4,3,1,0,2:T(8,128)}, u32[]{:S(2)}, u32[]{:S(2)}) %all-to-all-start) | async-done | bytes 4194336 | tf_op jit(solution)/shard_map/all_to_all | solution.py:84
  170.2 2.9 fusion.4
  173.5 8.5 %all_gather.11 = bf16[256,1024]{0,1:T(8,128)(2,1)S(1)} all-gather(bf16[128,1024]{0,1:T(8,128)(2,1)S(1)} %bitcast.200), channel_id=1, replica_groups=mesh['groups'=2,'seq'=8,'side'=1,'req'=2] {'req'}, dimensions={0}, use_global_device_ids=true | all-gather | bytes 786432 | tf_op jit(solution)/shard_map/all_gather | solution.py:94
  181.9 4.8 %fusion.96 = f32[256,2048]{1,0:T(8,128)} fusion(bf16[256,1024]{0,1:T(8,128)(2,1)S(1)} %all_gather.11, bf16[1024,2048]{1,0:T(8,128)(2,1)} %bitcast.212), kind=kOutput, calls=%fused_computation.149 | convolution fusion | flops 1073741824 | bytes 6815744 | tf_op jit(solution)/shard_map/dot_general | solution.py:97
  188.9 33.4 %reduce-scatter.2.cloned.1.call-done = f32[32,2048]{1,0:T(8,128)} async-done(((f32[256,2048]{1,0:T(8,128)}), f32[32,2048]{1,0:T(8,128)}) %reduce-scatter.2.cloned.1.call-update) | async-done | bytes 262160 | tf_op jit(solution)/shard_map/reduce_scatter | solution.py:96
  223.3 1.8 convolution_convert_fusion
  225.1 2.5 reshape.65
  228.5 40.2 %all_to_all.64 = bf16[8,8,6,2048]{3,1,2,0:T(8,128)(2,1)S(1)} all-to-all(bf16[8,8,6,2048]{3,1,2,0:T(8,128)(2,1)S(1)} %copy.144), channel_id=1, replica_groups=mesh['groups'=2,'seq'=8,'side'=1,'req'=2] {'seq','side'}, dimensions={0} | all-to-all | bytes 3145728 | tf_op jit(solution)/shard_map/all_to_all | solution.py:119
  268.8 14.8 %fusion.12 = f32[8,8,6,1024]{3,0,2,1:T(8,128)} fusion(bf16[8,2048,1024]{2,1,0:T(8,128)(2,1)} %param.20, bf16[8,8,6,2048]{3,1,2,0:T(8,128)(2,1)S(1)} %all_to_all.64), kind=kOutput, calls=%fused_computation.13 | convolution fusion | flops 1610612736 | bytes 36700160 | tf_op jit(solution)/shard_map/sekd,edf->sekf/dot_general | solution.py:117
  283.6 50.5 %all-reduce.2.cloned.1.call-done = f32[8,8,6,1024]{3,0,2,1:T(8,128)} async-done(((f32[8,8,6,1024]{3,0,2,1:T(8,128)}), f32[8,8,6,1024]{3,0,2,1:T(8,128)}) %all-reduce.2.cloned.1.call-update) | async-done | bytes 1572880 | tf_op jit(solution)/shard_map/psum | solution.py:123
  334.1 16.9 %fusion.8 = bf16[8,8,6,2048]{3,0,2,1:T(8,128)(2,1)S(1)} fusion(bf16[8,1024,2048]{2,1,0:T(8,128)(2,1)} %param.21, f32[8,8,6,1024]{3,0,2,1:T(8,128)} %all-reduce.2.cloned.1.call-done), kind=kOutput, calls=%fused_computation.9 | convolution fusion | flops 1613365248 | bytes 36700160 | tf_op jit(solution)/shard_map/sekf,efd->sekd/dot_general | solution.py:125
  351.0 2.0 copy.146
  353.0 4.7 %all-to-all-start.4 = ((bf16[8,8,6,2048]{3,1,2,0:T(8,128)(2,1)}), bf16[8,8,6,2048]{3,1,2,0:T(8,128)(2,1)}, u32[]{:S(2)}, u32[]{:S(2)}) async-start(bf16[8,8,6,2048]{3,1,2,0:T(8,128)(2,1)} %copy.146), calls=%async_computation.5 | async-start | bytes 3145728 | tf_op jit(solution)/shard_map/all_to_all | solution.py:128
  358.0 37.6 %all-to-all-done.4 = bf16[8,8,6,2048]{3,1,2,0:T(8,128)(2,1)} async-done(((bf16[8,8,6,2048]{3,1,2,0:T(8,128)(2,1)}), bf16[8,8,6,2048]{3,1,2,0:T(8,128)(2,1)}, u32[]{:S(2)}, u32[]{:S(2)}) %all-to-all-start.4) | async-done | bytes 1572896 | tf_op jit(solution)/shard_map/all_to_all | solution.py:128
  395.6 2.3 copy.147
  399.4 2.9 convolution_convert_fusion.1
  (121 shorter events, 26.4 us)
Async XLA Ops:
  7.2 5.2 %copy-start.26 = (bf16[1,16,512]{2,1,0:T(8,128)(2,1)S(1)}, bf16[1,16,512]{2,1,0:T(8,128)(2,1)}, u32[]{:S(2)}) copy-start(bf16[1,16,512]{2,1,0:T(8,128)(2,1)} %param.15) | copy-start | bytes 49156
  7.2 5.8 %copy-start.27 = (bf16[1,16,512]{2,1,0:T(8,128)(2,1)S(1)}, bf16[1,16,512]{2,1,0:T(8,128)(2,1)}, u32[]{:S(2)}) copy-start(bf16[1,16,512]{2,1,0:T(8,128)(2,1)} %param.16) | copy-start | bytes 49156
  7.2 6.4 %copy-start.12 = (bf16[1,128,512]{2,1,0:T(8,128)(2,1)S(1)}, bf16[1,128,512]{2,1,0:T(8,128)(2,1)}, u32[]{:S(2)}) copy-start(bf16[1,128,512]{2,1,0:T(8,128)(2,1)} %param.13) | copy-start | bytes 393220
  7.2 7.0 %copy-start.13 = (bf16[1,128,512]{2,1,0:T(8,128)(2,1)S(1)}, bf16[1,128,512]{2,1,0:T(8,128)(2,1)}, u32[]{:S(2)}) copy-start(bf16[1,128,512]{2,1,0:T(8,128)(2,1)} %param.14) | copy-start | bytes 393220
  7.2 34.3 %all-gather.3.cloned.1.call-start = ((), (), s32[]{:S(2)}) async-start(), calls=%async_computation.8 | async-start | bytes 2359296 | tf_op jit(solution)/shard_map/all_gather | solution.py:41
  12.3 32.7 %copy-start.4 = (pred[128,144]{0,1:T(8,128)(4,1)}, pred[128,144]{0,1:T(8,128)(4,1)S(1)}, u32[]{:S(2)}) copy-start(pred[128,144]{0,1:T(8,128)(4,1)S(1)} %pad_add_fusion) | copy-start | bytes 55300
  47.3 2.2 copy-start
  47.3 2.2 copy-start.8
  50.1 10.8 %all-to-all-start.2 = ((f32[1,4,16,128]{3,1,0,2:T(4,128)}), f32[1,4,16,128]{3,1,0,2:T(4,128)}, u32[]{:S(2)}, u32[]{:S(2)}) async-start(f32[1,4,16,128]{3,1,0,2:T(4,128)} %maximum_bitcast_fusion.18), calls=%async_computation.2 | async-start | bytes 65536 | tf_op jit(solution)/shard_map/all_to_all | solution.py:86
  54.1 2.5 copy-start.1
  54.1 2.4 copy-start.6
  54.1 2.4 copy-start.9
  54.1 2.4 copy-start.19
  54.1 2.4 copy-start.22
  57.1 1.7 copy-start.11
  57.1 1.7 copy-start.17
  58.8 7.1 %copy-start.2 = (f32[1,16,128,128]{3,2,1,0:T(8,128)S(1)}, f32[1,16,128,128]{3,2,1,0:T(8,128)}, u32[]{:S(2)}) copy-start(f32[1,16,128,128]{3,2,1,0:T(8,128)} %convolution_bitcast_fusion.2) | copy-start | bytes 3145732
  60.9 10.7 %all-to-all-start.1 = ((f32[1,4,16,128]{3,1,0,2:T(4,128)}), f32[1,4,16,128]{3,1,0,2:T(4,128)S(1)}, u32[]{:S(2)}, u32[]{:S(2)}) async-start(f32[1,4,16,128]{3,1,0,2:T(4,128)} %maximum_bitcast_fusion.17), calls=%async_computation.1 | async-start | bytes 65536 | tf_op jit(solution)/shard_map/all_to_all | solution.py:85
  71.7 98.5 %all-to-all-start = ((f32[1,4,16,128,128]{4,3,1,0,2:T(8,128)}), f32[1,4,16,128,128]{4,3,1,0,2:T(8,128)}, u32[]{:S(2)}, u32[]{:S(2)}) async-start(f32[1,4,16,128,128]{4,3,1,0,2:T(8,128)} %copy.134), calls=%async_computation | async-start | bytes 8388608 | tf_op jit(solution)/shard_map/all_to_all | solution.py:84
  76.2 146.2 %reduce-scatter.2.cloned.1.call-start = ((), (), s32[]{:S(2)}) async-start(), calls=%async_computation.6 | async-start | bytes 2359296 | tf_op jit(solution)/shard_map/reduce_scatter | solution.py:96
  186.8 147.3 %all-reduce.2.cloned.1.call-start = ((), (), s32[]{:S(2)}) async-start(), calls=%async_computation.7 | async-start | bytes 3145728 | tf_op jit(solution)/shard_map/psum | solution.py:123
  223.3 4.3 %copy-start.7 = (bf16[32,2048]{1,0:T(8,128)(2,1)}, bf16[32,2048]{1,0:T(8,128)(2,1)S(1)}, u32[]{:S(2)}) copy-start(bf16[32,2048]{1,0:T(8,128)(2,1)S(1)} %convert_element_type.59) | copy-start | bytes 393220
  353.0 4.7 %copy-start.29 = (f32[32,8]{0,1:T(8,128)S(1)}, f32[32,8]{0,1:T(8,128)}, u32[]{:S(2)}) copy-start(f32[32,8]{0,1:T(8,128)} %param.23) | copy-start | bytes 3076
  353.0 42.6 %all-to-all-start.4 = ((bf16[8,8,6,2048]{3,1,2,0:T(8,128)(2,1)}), bf16[8,8,6,2048]{3,1,2,0:T(8,128)(2,1)}, u32[]{:S(2)}, u32[]{:S(2)}) async-start(bf16[8,8,6,2048]{3,1,2,0:T(8,128)(2,1)} %copy.146), calls=%async_computation.5 | async-start | bytes 3145728 | tf_op jit(solution)/shard_map/all_to_all | solution.py:128
  (13 other events, 14.2 us)
Sparse Core Ops, SparseCore 0:
  9.6 31.8 all-gather.2
  186.9 35.4 reduce-scatter.1
  283.7 50.3 all-reduce.1
